TPU v7x, 32 devices: a whole 2x2x4 slice. The times are simulated.
32 devices in a mesh: expert: 4 (over x, core), tensor: 8 (over z, y).
Axes of the slice: x: 2, y: 2, z: 4, core: 2. Of those that a mesh axis runs over, the one named last changes fastest.
Arguments:
- tokens: bfloat16 [128, 7168], P('expert', 'tensor'), may hold values from -6 to 6
- routes: int32 [128, 8], P('expert'), may hold values from 0 to 15, all different within a row; in each aligned block of 128 rows (0 to 127, 128 to 255, ...) at most 128 rows name the same one
- gates: bfloat16 [128, 8], P('expert'), may hold values from 0.099609375 to 0.59765625
- w_gate: bfloat16 [16, 2048, 7168], P('expert', 'tensor'), may hold values from -0.0625 to 0.0625
- w_up: bfloat16 [16, 2048, 7168], P('expert', 'tensor'), may hold values from -0.0625 to 0.0625
- w_down: bfloat16 [16, 2048, 7168], P('expert', None, 'tensor'), may hold values from -0.125 to 0.125
Outputs:
- moe_out: bfloat16 [128, 7168], P('expert', 'tensor')
Inputs may be any that keep to these rules, and one draw needn't show every extreme that they name: `routes`: each row names 8 different experts. No expert is named by more than 128 of the 128 rows, and one expert is named by exactly 128 rows.
All inputs are finite; a program needn't handle non-finite values.
Results may differ from a plain program's by a relative error of at most 0.0049.
Values may be sent and summed in bfloat16 or wider, within the bound.
A program may use at most 128 MiB of HBM per device.

v0:
```python
import jax
import jax.numpy as jnp
from jax import lax
from jax.sharding import PartitionSpec as P

CAP = 128


def entering(value, axis, combine, identity):
    length, index = (lax.axis_size(axis), lax.axis_index(axis))
    everything = lax.all_gather(value, axis)
    start = jnp.broadcast_to(jnp.asarray(identity, value.dtype), value.shape)

    def lap(k, before):
        reached = k < index
        new = combine(before, everything[k])
        return jnp.where(reached, new, before)

    return lax.fori_loop(0, length, lap, start)


def add_counts(earlier, later):
    return earlier + later


def on_device(tokens, routes, gates, w_gate, w_up, w_down):
    exp_dev = w_gate.shape[0]
    experts = exp_dev * lax.axis_size("expert")
    group_index = lax.axis_index("expert")
    expert_ids = jnp.arange(experts, dtype=jnp.int32)
    route_hits = routes[:, :, None] == expert_ids[None, None, :]
    member = jnp.sum(route_hits.astype(jnp.int32), axis=1)
    counts = jnp.sum(member, axis=0)
    offset = entering(counts, "expert", add_counts, jnp.zeros_like(counts))
    before = jnp.cumsum(member, axis=0) - member + offset[None, :]
    own_slot = jnp.sum(jnp.where(route_hits, before[:, None, :], 0), axis=2).astype(jnp.int32)
    all_routes, all_slots = (
        lax.all_gather(routes, "expert", axis=0, tiled=True),
        lax.all_gather(own_slot, "expert", axis=0, tiled=True),
    )
    row_block, all_gates = (
        lax.all_gather(tokens, "expert", axis=0, tiled=True),
        lax.all_gather(gates, "expert", axis=0, tiled=True),
    )
    gathered = lax.all_gather(row_block, "tensor", axis=1, tiled=True)
    local_ids = all_routes - group_index * exp_dev
    is_local = (local_ids >= 0) & (local_ids < exp_dev)
    slot_id = jnp.where(is_local, local_ids * CAP + all_slots, -1)
    slot_range = jnp.arange(exp_dev * CAP, dtype=jnp.int32)
    matches = slot_id[:, :, None] == slot_range[None, None, :]
    picked = jnp.any(matches, axis=1).astype(jnp.bfloat16)
    mixing = jnp.sum(jnp.where(matches, all_gates.astype(jnp.float32)[:, :, None], 0.0), axis=1)
    slot_rows = lax.dot_general(
        picked, gathered, (((0,), (0,)), ((), ())), preferred_element_type=jnp.float32
    ).astype(jnp.bfloat16)
    slot_rows = slot_rows.reshape(exp_dev, CAP, gathered.shape[1])
    gate_proj = jnp.einsum("ecd,efd->ecf", slot_rows, w_gate, preferred_element_type=jnp.float32)
    up_proj = jnp.einsum("ecd,efd->ecf", slot_rows, w_up, preferred_element_type=jnp.float32)
    hidden = (jax.nn.silu(gate_proj) * up_proj).astype(jnp.bfloat16)
    expert_out = jnp.einsum(
        "ecf,efd->ecd",
        lax.all_gather(hidden, "tensor", axis=2, tiled=True),
        w_down,
        preferred_element_type=jnp.float32,
    )
    expert_out = expert_out.reshape(exp_dev * CAP, w_down.shape[2])
    partial_value = jnp.dot(mixing, expert_out, precision=lax.Precision.HIGHEST)
    result = lax.psum_scatter(partial_value, "expert", scatter_dimension=0, tiled=True)
    return result.astype(jnp.bfloat16)


def solution(mesh):
    placed = (
        P("expert", "tensor"),
        P("expert", None),
        P("expert", None),
        P("expert", "tensor", None),
        P("expert", "tensor", None),
        P("expert", None, "tensor"),
    )
    return jax.shard_map(
        on_device, mesh=mesh, in_specs=placed, out_specs=P("expert", "tensor"), check_vma=False
    )
```

profile of v0, /device:TPU:0, one launch (start us, length us, event | category | flops | bytes accessed | tf_op | source)
XLA Modules:
  0.0 181.3 jit_solution(15544654380891682984)
XLA Ops:
  6.5 8.7 %all_gather.29 = bf16[128,896]{1,0:T(8,128)(2,1)} all-gather(bf16[32,896]{1,0:T(8,128)(2,1)} %param.8), channel_id=1, replica_groups=mesh['expert'=4,'tensor'=8] {'expert'}, dimensions={0}, use_global_device_ids=true | all-gather | bytes 286720 | tf_op jit(solution)/shard_map/all_gather | solution.py:42
  15.3 1.2 dynamic-slice
  17.2 0.8 convert_reduce_fusion
  18.0 0.2 dynamic-update-slice
  18.2 4.3 %all-reduce = s32[64]{0:T(128)S(1)} all-reduce(s32[64]{0:T(128)S(1)} %dynamic-update-slice), channel_id=2, replica_groups=mesh['expert'=4,'tensor'=8] {'expert'}, use_global_device_ids=true, to_apply=%add | all-reduce | flops 64 | bytes 512
  22.5 0.1 reshape.32
  22.7 0.1 while.14
  22.9 0.7 select_reduce_fusion.1
  23.7 5.2 %all-gather.2 = s32[4,32,8]{1,2,0:T(8,128)S(1)} all-gather(s32[1,32,8]{1,2,0:T(8,128)S(1)} %bitcast.29), channel_id=1, replica_groups=mesh['expert'=4,'tensor'=8] {'expert'}, dimensions={0}, use_global_device_ids=true | all-gather | bytes 5120 | tf_op jit(solution)/shard_map/all_gather | solution.py:39
  28.9 5.3 %all-gather.1 = s32[4,32,8]{1,2,0:T(8,128)S(1)} all-gather(s32[1,32,8]{1,2,0:T(8,128)} %bitcast.28), channel_id=1, replica_groups=mesh['expert'=4,'tensor'=8] {'expert'}, dimensions={0}, use_global_device_ids=true | all-gather | bytes 5120 | tf_op jit(solution)/shard_map/all_gather | solution.py:38
  34.2 0.1 copy.25
  34.3 0.7 fusion
  35.0 27.3 %all-gather.7.cloned.1.call-done = bf16[128,7168]{1,0:T(8,128)(2,1)} async-done(((bf16[128,896]{1,0:T(8,128)(2,1)}), bf16[128,7168]{1,0:T(8,128)(2,1)}) %all-gather.7.cloned.1.call-update) | async-done | bytes 1835024 | tf_op jit(solution)/shard_map/all_gather | solution.py:45
  62.3 6.6 %convolution_convert_fusion = bf16[512,7168]{1,0:T(8,128)(2,1)} fusion(pred[128,512]{1,0:T(8,128)(4,1)S(1)} %fusion, bf16[128,7168]{1,0:T(8,128)(2,1)} %all-gather.7.cloned.1.call-done), kind=kOutput, calls=%fused_computation.2 | convolution fusion | flops 943194112 | bytes 9240576 | tf_op jit(solution)/shard_map/dot_general | solution.py:53
  68.9 12.3 %fusion.2 = f32[4,128,256]{2,1,0:T(8,128)S(1)} fusion(bf16[4,128,7168]{2,1,0:T(8,128)(2,1)} %bitcast.22, bf16[4,256,7168]{2,1,0:T(8,128)(2,1)} %param.11), kind=kOutput, calls=%fused_computation.14 | convolution fusion | flops 1879048192 | bytes 22544384 | tf_op jit(solution)/shard_map/ecd,efd->ecf/dot_general | solution.py:57
  81.2 13.0 %fusion.1 = bf16[4,128,256]{2,1,0:T(8,128)(2,1)} fusion(bf16[4,128,7168]{2,1,0:T(8,128)(2,1)} %bitcast.23, bf16[4,256,7168]{2,1,0:T(8,128)(2,1)} %param.12, f32[4,128,256]{2,1,0:T(8,128)S(1)} %fusion.2), kind=kOutput, calls=%fused_computation.7 | convolution fusion | flops 1879834624 | bytes 22806528 | tf_op jit(solution)/shard_map/ecd,efd->ecf/dot_general | solution.py:58
  94.3 5.4 %all-gather.3 = bf16[4,32,8]{1,2,0:T(8,128)(2,1)S(1)} all-gather(bf16[1,32,8]{1,2,0:T(8,128)(2,1)S(1)} %bitcast.30), channel_id=1, replica_groups=mesh['expert'=4,'tensor'=8] {'expert'}, dimensions={0}, use_global_device_ids=true | all-gather | bytes 2560 | tf_op jit(solution)/shard_map/all_gather | solution.py:43
  99.6 0.1 copy.26
  99.7 0.7 select_reduce_fusion
  100.4 43.1 %all-gather.9.cloned.1.call-done = bf16[4,128,2048]{2,1,0:T(8,128)(2,1)} async-done(((bf16[4,128,256]{2,1,0:T(8,128)(2,1)}), bf16[4,128,2048]{2,1,0:T(8,128)(2,1)}) %all-gather.9.cloned.1.call-update) | async-done | bytes 2097168 | tf_op jit(solution)/shard_map/all_gather | solution.py:62
  143.5 8.2 %fusion.3 = f32[4,128,896]{2,1,0:T(8,128)S(1)} fusion(bf16[4,128,2048]{2,1,0:T(8,128)(2,1)} %all-gather.9.cloned.1.call-done, bf16[4,2048,896]{2,1,0:T(8,128)(2,1)} %param.13), kind=kOutput, calls=%fused_computation.15 | convolution fusion | flops 1879048192 | bytes 18612224 | tf_op jit(solution)/shard_map/ecf,efd->ecd/dot_general | solution.py:60
  151.7 2.0 %fusion.4 = f32[128,896]{1,0:T(8,128)} fusion(f32[128,512]{1,0:T(8,128)S(1)} %select_reduce_fusion, f32[512,896]{1,0:T(8,128)S(1)} %bitcast.24), kind=kOutput, calls=%fused_computation.16 | convolution fusion | flops 704643072 | bytes 2555904 | tf_op jit(solution)/shard_map/dot_general | solution.py:67
  153.7 19.5 %reduce-scatter.2.cloned.1.call-done = f32[32,896]{1,0:T(8,128)} async-done(((f32[128,896]{1,0:T(8,128)}), f32[32,896]{1,0:T(8,128)}) %reduce-scatter.2.cloned.1.call-update) | async-done | bytes 114704 | tf_op jit(solution)/shard_map/reduce_scatter | solution.py:68
  173.2 1.5 convert_element_type.20
  (19 shorter events, 0.4 us)
Async XLA Ops:
  6.5 55.8 %all-gather.7.cloned.1.call-start = ((), (), s32[]{:S(2)}) async-start(), calls=%async_computation.1 | async-start | bytes 2064384 | tf_op jit(solution)/shard_map/all_gather | solution.py:45
  15.3 128.3 %all-gather.9.cloned.1.call-start = ((), (), s32[]{:S(2)}) async-start(), calls=%async_computation.2 | async-start | bytes 2359296 | tf_op jit(solution)/shard_map/all_gather | solution.py:62
  81.2 13.1 %copy-start = (bf16[32,8]{0,1:T(8,128)(2,1)S(1)}, bf16[32,8]{0,1:T(8,128)(2,1)}, u32[]{:S(2)}) copy-start(bf16[32,8]{0,1:T(8,128)(2,1)} %param.10) | copy-start | bytes 1540
  94.2 79.0 %reduce-scatter.2.cloned.1.call-start = ((), (), s32[]{:S(2)}) async-start(), calls=%async_computation.3 | async-start | bytes 573440 | tf_op jit(solution)/shard_map/reduce_scatter | solution.py:68
Sparse Core Ops, SparseCore 0:
  15.4 46.8 all-gather.6
  94.3 49.1 all-gather.8
  153.8 19.3 reduce-scatter.1
where the time goes:
time: 182 us; the launch traced here: 181 us
  waiting for transfers between devices  90 us (49%)
  matrix products  42 us (23%)
  blocking collectives  28.9 us (16%)
  between operations  13.8 us (8%)
  other arithmetic  4.59 us (3%)
  local copies, waits for them, and re-layouts  1.88 us (1%)
    all_gather x1, waiting for transfers between devices, on_device(): lax.all_gather(hidden, 'tensor', axis=2, tiled=True)  43.1 us
    all_gather x1, waiting for transfers between devices, on_device(): gathered = lax.all_gather(row_block, 'tensor', axis=1, tiled=True)  27.3 us
    reduce_scatter x1, waiting for transfers between devices, on_device(): lax.psum_scatter(partial_value, 'expert', scatter_dimension=0, tiled=True)  19.5 us
    dot_general x1, matrix products, on_device(): jnp.einsum('ecd,efd->ecf', slot_rows, w_up, preferred_element_type=jnp.fl...  13 us
    dot_general x1, matrix products, on_device(): jnp.einsum('ecd,efd->ecf', slot_rows, w_gate, preferred_element_type=jnp....  12.3 us
    all_gather x1, blocking collectives, on_device(): lax.all_gather(tokens, 'expert', axis=0, tiled=True)  8.71 us
    dot_general x1, matrix products, on_device(): jnp.einsum('ecf,efd->ecd', lax.all_gather(hidden, 'tensor', axis=2, tiled...  8.16 us
    dot_general x1, matrix products, on_device(): lax.dot_general(picked, gathered, (((0,), (0,)), ((), ())), preferred_ele...  6.58 us
  transfers between devices with their start and end apart: 3, of which 3 were waited for; matrix products, arithmetic and copies ran while one was open for 3% of the time, Pallas kernels for 0%

commit v1 on v0

--- a/solution.py
+++ b/solution.py
@@ -57,12 +57,41 @@
     gate_proj = jnp.einsum("ecd,efd->ecf", slot_rows, w_gate, preferred_element_type=jnp.float32)
     up_proj = jnp.einsum("ecd,efd->ecf", slot_rows, w_up, preferred_element_type=jnp.float32)
     hidden = (jax.nn.silu(gate_proj) * up_proj).astype(jnp.bfloat16)
+    n_now = lax.axis_size("tensor")
+    y2 = lax.axis_index("tensor")
+    mat_out, formed, tmp = (n_now, y2, hidden.shape[2])
+    column = tuple(((p, (p + 1) % mat_out) for p in range(mat_out)))
+    top = mat_out // 2
+    spare = small = hidden
     expert_out = jnp.einsum(
         "ecf,efd->ecd",
-        lax.all_gather(hidden, "tensor", axis=2, tiled=True),
-        w_down,
+        hidden,
+        lax.dynamic_slice_in_dim(w_down, formed * tmp, hidden.shape[2], axis=1),
         preferred_element_type=jnp.float32,
     )
+    runs = tuple(((p, (p - 1) % mat_out) for p in range(mat_out)))
+    for num in tuple(range(1, top + 1)):
+        spare = lax.ppermute(spare, axis_name="tensor", perm=column)
+        if num < mat_out - top:
+            small = lax.ppermute(small, axis_name="tensor", perm=runs)
+            w1 = jnp.einsum(
+                "ecf,efd->ecd",
+                small,
+                lax.dynamic_slice_in_dim(
+                    w_down, (formed + num) % mat_out * tmp, small.shape[2], axis=1
+                ),
+                preferred_element_type=jnp.float32,
+            )
+            expert_out = expert_out + w1
+        e_next = jnp.einsum(
+            "ecf,efd->ecd",
+            spare,
+            lax.dynamic_slice_in_dim(
+                w_down, (formed - num) % mat_out * tmp, spare.shape[2], axis=1
+            ),
+            preferred_element_type=jnp.float32,
+        )
+        expert_out = expert_out + e_next
     expert_out = expert_out.reshape(exp_dev * CAP, w_down.shape[2])
     partial_value = jnp.dot(mixing, expert_out, precision=lax.Precision.HIGHEST)
     result = lax.psum_scatter(partial_value, "expert", scatter_dimension=0, tiled=True)

time: 182 us -> 175 us (0.962)
  waiting for transfers between devices: 90 us -> 66.1 us
  starting transfers between devices: 0.09 us -> 9.37 us
  matrix products: 42 us -> 49.1 us
    all_gather x1 -> x0, waiting for transfers between devices: 43.1 us -> none  [on_device(): lax.all_gather(hidden, 'tensor', axis=2, tiled=True)]
    ppermute x0 -> x7, waiting for transfers between devices: none -> 25.6 us  [the longest x3 14.7 us: on_device(): small = lax.ppermute(small, axis_name='tensor', perm=runs)]
    ppermute x0 -> x7, starting transfers between devices: none -> 9.33 us  [the longest x3 6 us: on_device(): small = lax.ppermute(small, axis_name='tensor', perm=runs)]
    dot_general x1 -> x8, matrix products: 8.16 us -> 16 us  [the longest x4 8.19 us: on_device(): jnp.einsum('ecf,efd->ecd', spare, lax.dynamic_slice_in_dim(w_down, (forme...]
    all_gather x1, waiting for transfers between devices: 27.3 us -> 21.1 us  [on_device(): gathered = lax.all_gather(row_block, 'tensor', axis=1, tiled=True)]
  transfers between devices with their start and end apart: 3 -> 9, of which waited for: 3 -> 6; matrix products, arithmetic and copies ran while one was open for 3% -> 11% of each run, Pallas kernels for 0% -> 0%
where the time goes in v1:
time: 175 us; the launch traced here: 174 us
  waiting for transfers between devices  66.1 us (38%)
  matrix products  49.1 us (28%)
  blocking collectives  28.8 us (16%)
  between operations  14.3 us (8%)
  starting transfers between devices  9.37 us (5%)
  other arithmetic  4.59 us (3%)
  local copies, waits for them, and re-layouts  1.88 us (1%)
    all_gather x1, waiting for transfers between devices, on_device(): gathered = lax.all_gather(row_block, 'tensor', axis=1, tiled=True)  21.1 us
    reduce_scatter x1, waiting for transfers between devices, on_device(): lax.psum_scatter(partial_value, 'expert', scatter_dimension=0, tiled=True)  19.4 us
    ppermute x3, waiting for transfers between devices, on_device(): small = lax.ppermute(small, axis_name='tensor', perm=runs)  14.7 us
    dot_general x1, matrix products, on_device(): jnp.einsum('ecd,efd->ecf', slot_rows, w_up, preferred_element_type=jnp.fl...  12.3 us
    dot_general x1, matrix products, on_device(): jnp.einsum('ecd,efd->ecf', slot_rows, w_gate, preferred_element_type=jnp....  12.3 us
    ppermute x4, waiting for transfers between devices, on_device(): spare = lax.ppermute(spare, axis_name='tensor', perm=column)  10.9 us
    all_gather x1, blocking collectives, on_device(): lax.all_gather(tokens, 'expert', axis=0, tiled=True)  8.71 us
    dot_general x4, matrix products, on_device(): jnp.einsum('ecf,efd->ecd', spare, lax.dynamic_slice_in_dim(w_down, (forme...  8.19 us
  transfers between devices with their start and end apart: 9, of which 6 were waited for; matrix products, arithmetic and copies ran while one was open for 11% of the time, Pallas kernels for 0%

profile of v1, /device:TPU:0, one launch (start us, length us, event | category | flops | bytes accessed | tf_op | source)
XLA Modules:
  0.0 174.3 jit_solution(17121791736678623432)
XLA Ops:
  6.5 8.7 %all_gather.26 = bf16[128,896]{1,0:T(8,128)(2,1)} all-gather(bf16[32,896]{1,0:T(8,128)(2,1)} %param.8), channel_id=1, replica_groups=mesh['expert'=4,'tensor'=8] {'expert'}, dimensions={0}, use_global_device_ids=true | all-gather | bytes 286720 | tf_op jit(solution)/shard_map/all_gather | solution.py:42
  18.3 4.3 %all-reduce = s32[64]{0:T(128)S(1)} all-reduce(s32[64]{0:T(128)S(1)} %dynamic-update-slice), channel_id=2, replica_groups=mesh['expert'=4,'tensor'=8] {'expert'}, use_global_device_ids=true, to_apply=%add | all-reduce | flops 64 | bytes 512
  23.8 5.2 %all-gather.2 = s32[4,32,8]{1,2,0:T(8,128)S(1)} all-gather(s32[1,32,8]{1,2,0:T(8,128)S(1)} %bitcast.35), channel_id=1, replica_groups=mesh['expert'=4,'tensor'=8] {'expert'}, dimensions={0}, use_global_device_ids=true | all-gather | bytes 5120 | tf_op jit(solution)/shard_map/all_gather | solution.py:39
  29.0 5.3 %all-gather.1 = s32[4,32,8]{1,2,0:T(8,128)S(1)} all-gather(s32[1,32,8]{1,2,0:T(8,128)} %bitcast.34), channel_id=1, replica_groups=mesh['expert'=4,'tensor'=8] {'expert'}, dimensions={0}, use_global_device_ids=true | all-gather | bytes 5120 | tf_op jit(solution)/shard_map/all_gather | solution.py:38
  34.4 5.3 %all-gather.3 = bf16[4,32,8]{1,2,0:T(8,128)(2,1)S(1)} all-gather(bf16[1,32,8]{1,2,0:T(8,128)(2,1)} %bitcast.36), channel_id=1, replica_groups=mesh['expert'=4,'tensor'=8] {'expert'}, dimensions={0}, use_global_device_ids=true | all-gather | bytes 2560 | tf_op jit(solution)/shard_map/all_gather | solution.py:43
  41.3 21.1 %all-gather.6.cloned.1.call-done = bf16[128,7168]{1,0:T(8,128)(2,1)} async-done(((bf16[128,896]{1,0:T(8,128)(2,1)}), bf16[128,7168]{1,0:T(8,128)(2,1)}) %all-gather.6.cloned.1.call-update) | async-done | bytes 1835024 | tf_op jit(solution)/shard_map/all_gather | solution.py:45
  62.3 6.6 %convolution_convert_fusion = bf16[512,7168]{1,0:T(8,128)(2,1)} fusion(pred[128,512]{1,0:T(8,128)(4,1)S(1)} %fusion, bf16[128,7168]{1,0:T(8,128)(2,1)} %all-gather.6.cloned.1.call-done), kind=kOutput, calls=%fused_computation.2 | convolution fusion | flops 943194112 | bytes 9240576 | tf_op jit(solution)/shard_map/dot_general | solution.py:53
  68.9 12.3 %fusion.28 = f32[4,128,256]{2,1,0:T(8,128)S(1)} fusion(bf16[4,128,7168]{2,1,0:T(8,128)(2,1)} %bitcast.28, bf16[4,256,7168]{2,1,0:T(8,128)(2,1)} %param.11), kind=kOutput, calls=%fused_computation.39 | convolution fusion | flops 1879048192 | bytes 22544384 | tf_op jit(solution)/shard_map/ecd,efd->ecf/dot_general | solution.py:57
  81.2 12.3 %fusion.19 = bf16[4,128,256]{2,1,0:T(8,128)(2,1)S(1)} fusion(bf16[4,128,7168]{2,1,0:T(8,128)(2,1)} %bitcast.29, bf16[4,256,7168]{2,1,0:T(8,128)(2,1)} %param.12, f32[4,128,256]{2,1,0:T(8,128)S(1)} %fusion.28), kind=kOutput, calls=%fused_computation.24 | convolution fusion | flops 1879834624 | bytes 22806528 | tf_op jit(solution)/shard_map/ecd,efd->ecf/dot_general | solution.py:58
  93.5 2.2 %collective-permute-start = (bf16[4,128,256]{2,1,0:T(8,128)(2,1)S(1)}, bf16[4,128,256]{2,1,0:T(8,128)(2,1)S(1)}, u32[]{:S(2)}, u32[]{:S(2)}) collective-permute-start(bf16[4,128,256]{2,1,0:T(8,128)(2,1)S(1)} %fusion.19), channel_id=1, source_target_pairs={{0,7},{1,0},{2,1},{3,2},{4,3},{5,4},{6,5},{7,6},{8,15},{9,8},{10,9... | collective-permute-start | bytes 786440 | tf_op jit(solution)/shard_map/ppermute | solution.py:76
  95.7 2.0 %fusion.15 = f32[4,128,896]{2,1,0:T(8,128)S(1)} fusion(bf16[4,128,256]{2,1,0:T(8,128)(2,1)S(1)} %fusion.19, bf16[4,2048,896]{2,1,0:T(8,128)(2,1)} %param.13, s32[]{:T(128)S(6)} %select_n.91), kind=kOutput, calls=%fused_computation.21 | convolution fusion | flops 234881024 | bytes 3932164 | tf_op jit(solution)/shard_map/ecf,efd->ecd/dot_general | solution.py:66
  97.6 8.3 %collective-permute-done = bf16[4,128,256]{2,1,0:T(8,128)(2,1)S(1)} collective-permute-done((bf16[4,128,256]{2,1,0:T(8,128)(2,1)S(1)}, bf16[4,128,256]{2,1,0:T(8,128)(2,1)S(1)}, u32[]{:S(2)}, u32[]{:S(2)}) %collective-permute-start) | collective-permute-done | bytes 262176 | tf_op jit(solution)/shard_map/ppermute | solution.py:76
  105.9 2.0 %collective-permute-start.2 = (bf16[4,128,256]{2,1,0:T(8,128)(2,1)S(1)}, bf16[4,128,256]{2,1,0:T(8,128)(2,1)S(1)}, u32[]{:S(2)}, u32[]{:S(2)}) collective-permute-start(bf16[4,128,256]{2,1,0:T(8,128)(2,1)S(1)} %collective-permute-done), channel_id=1, source_target_pairs={{0,7},{1,0},{2,1},{3,2},{4,3},{5,4},{6,5},{7,6},{8,15},{9,8},{10,9... | collective-permute-start | bytes 786440 | tf_op jit(solution)/shard_map/ppermute | solution.py:76
  110.2 2.0 %fusion.13 = f32[4,128,896]{2,1,0:T(8,128)S(1)} fusion(bf16[4,128,256]{2,1,0:T(8,128)(2,1)S(1)} %collective-permute-done, bf16[4,2048,896]{2,1,0:T(8,128)(2,1)} %param.13, s32[]{:T(128)S(6)} %select_n.93), kind=kOutput, calls=%fused_computation.19 | convolution fusion | flops 234881024 | bytes 3932164 | tf_op jit(solution)/shard_map/ecf,efd->ecd/dot_general | solution.py:77
  112.1 6.4 %collective-permute-done.2 = bf16[4,128,256]{2,1,0:T(8,128)(2,1)S(1)} collective-permute-done((bf16[4,128,256]{2,1,0:T(8,128)(2,1)S(1)}, bf16[4,128,256]{2,1,0:T(8,128)(2,1)S(1)}, u32[]{:S(2)}, u32[]{:S(2)}) %collective-permute-start.2) | collective-permute-done | bytes 262176 | tf_op jit(solution)/shard_map/ppermute | solution.py:76
  120.9 2.0 %fusion.7 = f32[4,128,896]{2,1,0:T(8,128)S(1)} fusion(bf16[4,128,256]{2,1,0:T(8,128)(2,1)S(1)} %collective-permute-done.3, bf16[4,2048,896]{2,1,0:T(8,128)(2,1)} %param.13, s32[]{:T(128)S(6)} %select_n.99), kind=kOutput, calls=%fused_computation.13 | convolution fusion | flops 234881024 | bytes 3932164 | tf_op jit(solution)/shard_map/ecf,efd->ecd/dot_general | solution.py:86
  122.9 2.0 %fusion.9 = f32[4,128,896]{2,1,0:T(8,128)S(1)} fusion(bf16[4,128,256]{2,1,0:T(8,128)(2,1)S(1)} %collective-permute-done.2, bf16[4,2048,896]{2,1,0:T(8,128)(2,1)} %param.13, s32[]{:T(128)S(6)} %select_n.97), kind=kOutput, calls=%fused_computation.15 | convolution fusion | flops 234881024 | bytes 3932164 | tf_op jit(solution)/shard_map/ecf,efd->ecd/dot_general | solution.py:77
  124.8 6.4 %collective-permute-done.5 = bf16[4,128,256]{2,1,0:T(8,128)(2,1)S(1)} collective-permute-done((bf16[4,128,256]{2,1,0:T(8,128)(2,1)S(1)}, bf16[4,128,256]{2,1,0:T(8,128)(2,1)S(1)}, u32[]{:S(2)}, u32[]{:S(2)}) %collective-permute-start.5) | collective-permute-done | bytes 262176 | tf_op jit(solution)/shard_map/ppermute | solution.py:74
  131.2 2.5 %collective-permute-start.6 = (bf16[4,128,256]{2,1,0:T(8,128)(2,1)S(1)}, bf16[4,128,256]{2,1,0:T(8,128)(2,1)S(1)}, u32[]{:S(2)}, u32[]{:S(2)}) collective-permute-start(bf16[4,128,256]{2,1,0:T(8,128)(2,1)S(1)} %collective-permute-done.5), channel_id=1, source_target_pairs={{0,1},{1,2},{2,3},{3,4},{4,5},{5,6},{6,7},{7,0},{8,9},{9,10},{10,1... | collective-permute-start | bytes 786440 | tf_op jit(solution)/shard_map/ppermute | solution.py:74
  135.7 2.0 %fusion.5 = f32[4,128,896]{2,1,0:T(8,128)S(1)} fusion(bf16[4,128,256]{2,1,0:T(8,128)(2,1)S(1)} %collective-permute-done.4, bf16[4,2048,896]{2,1,0:T(8,128)(2,1)} %param.13, s32[]{:T(128)S(6)} %select_n.101), kind=kOutput, calls=%fused_computation.11 | convolution fusion | flops 234881024 | bytes 3932164 | tf_op jit(solution)/shard_map/ecf,efd->ecd/dot_general | solution.py:77
  137.6 4.5 %collective-permute-done.6 = bf16[4,128,256]{2,1,0:T(8,128)(2,1)S(1)} collective-permute-done((bf16[4,128,256]{2,1,0:T(8,128)(2,1)S(1)}, bf16[4,128,256]{2,1,0:T(8,128)(2,1)S(1)}, u32[]{:S(2)}, u32[]{:S(2)}) %collective-permute-start.6) | collective-permute-done | bytes 262176 | tf_op jit(solution)/shard_map/ppermute | solution.py:74
  142.2 2.4 %add_add_fusion = f32[4,128,896]{2,1,0:T(8,128)S(1)} fusion(f32[4,128,896]{2,1,0:T(8,128)S(1)} %fusion.3, f32[4,128,896]{2,1,0:T(8,128)S(1)} %fusion.5, f32[4,128,896]{2,1,0:T(8,128)S(1)} %fusion.7, f32[4,128,896]{2,1,0:T(8,128)S(1)} %fusion.9, f32[4,128,896]{2,1,0:T(8,128)S(1)} %fusion.11, f32[4,128,896]{2,1,0:T(8,128)S(1)} %fusion.15, ...), kind=kOutput, calls=%fused_computation.8 | convolution fusion | flops 238092288 | bytes 16777220 | tf_op jit(solution)/shard_map/ecf,efd->ecd/dot_general | solution.py:86
  144.5 2.0 %fusion.29 = f32[128,896]{1,0:T(8,128)} fusion(f32[128,512]{1,0:T(8,128)S(1)} %select_reduce_fusion, f32[512,896]{1,0:T(8,128)S(1)} %bitcast.30), kind=kOutput, calls=%fused_computation.40 | convolution fusion | flops 704643072 | bytes 2555904 | tf_op jit(solution)/shard_map/dot_general | solution.py:96
  146.5 19.4 %reduce-scatter.2.cloned.1.call-done = f32[32,896]{1,0:T(8,128)} async-done(((f32[128,896]{1,0:T(8,128)}), f32[32,896]{1,0:T(8,128)}) %reduce-scatter.2.cloned.1.call-update) | async-done | bytes 114704 | tf_op jit(solution)/shard_map/reduce_scatter | solution.py:97
  (35 shorter events, 13.2 us)
Async XLA Ops:
  6.5 55.8 %all-gather.6.cloned.1.call-start = ((), (), s32[]{:S(2)}) async-start(), calls=%async_computation.1 | async-start | bytes 2064384 | tf_op jit(solution)/shard_map/all_gather | solution.py:45
  15.3 150.6 %reduce-scatter.2.cloned.1.call-start = ((), (), s32[]{:S(2)}) async-start(), calls=%async_computation.2 | async-start | bytes 573440 | tf_op jit(solution)/shard_map/reduce_scatter | solution.py:97
  93.5 12.4 %collective-permute-start = (bf16[4,128,256]{2,1,0:T(8,128)(2,1)S(1)}, bf16[4,128,256]{2,1,0:T(8,128)(2,1)S(1)}, u32[]{:S(2)}, u32[]{:S(2)}) collective-permute-start(bf16[4,128,256]{2,1,0:T(8,128)(2,1)S(1)} %fusion.19), channel_id=1, source_target_pairs={{0,7},{1,0},{2,1},{3,2},{4,3},{5,4},{6,5},{7,6},{8,15},{9,8},{10,9... | collective-permute-start | bytes 786440 | tf_op jit(solution)/shard_map/ppermute | solution.py:76
  95.7 12.3 %collective-permute-start.1 = (bf16[4,128,256]{2,1,0:T(8,128)(2,1)S(1)}, bf16[4,128,256]{2,1,0:T(8,128)(2,1)S(1)}, u32[]{:S(2)}, u32[]{:S(2)}) collective-permute-start(bf16[4,128,256]{2,1,0:T(8,128)(2,1)S(1)} %fusion.19), channel_id=1, source_target_pairs={{0,1},{1,2},{2,3},{3,4},{4,5},{5,6},{6,7},{7,0},{8,9},{9,10},{10,1... | collective-permute-start | bytes 786440 | tf_op jit(solution)/shard_map/ppermute | solution.py:74
  105.9 12.6 %collective-permute-start.2 = (bf16[4,128,256]{2,1,0:T(8,128)(2,1)S(1)}, bf16[4,128,256]{2,1,0:T(8,128)(2,1)S(1)}, u32[]{:S(2)}, u32[]{:S(2)}) collective-permute-start(bf16[4,128,256]{2,1,0:T(8,128)(2,1)S(1)} %collective-permute-done), channel_id=1, source_target_pairs={{0,7},{1,0},{2,1},{3,2},{4,3},{5,4},{6,5},{7,6},{8,15},{9,8},{10,9... | collective-permute-start | bytes 786440 | tf_op jit(solution)/shard_map/ppermute | solution.py:76
  107.9 12.4 %collective-permute-start.3 = (bf16[4,128,256]{2,1,0:T(8,128)(2,1)S(1)}, bf16[4,128,256]{2,1,0:T(8,128)(2,1)S(1)}, u32[]{:S(2)}, u32[]{:S(2)}) collective-permute-start(bf16[4,128,256]{2,1,0:T(8,128)(2,1)S(1)} %collective-permute-done.1), channel_id=1, source_target_pairs={{0,1},{1,2},{2,3},{3,4},{4,5},{5,6},{6,7},{7,0},{8,9},{9,10},{10,1... | collective-permute-start | bytes 786440 | tf_op jit(solution)/shard_map/ppermute | solution.py:74
  118.6 17.1 %collective-permute-start.4 = (bf16[4,128,256]{2,1,0:T(8,128)(2,1)S(1)}, bf16[4,128,256]{2,1,0:T(8,128)(2,1)S(1)}, u32[]{:S(2)}, u32[]{:S(2)}) collective-permute-start(bf16[4,128,256]{2,1,0:T(8,128)(2,1)S(1)} %collective-permute-done.2), channel_id=1, source_target_pairs={{0,7},{1,0},{2,1},{3,2},{4,3},{5,4},{6,5},{7,6},{8,15},{9,8},{10,9... | collective-permute-start | bytes 786440 | tf_op jit(solution)/shard_map/ppermute | solution.py:76
  120.3 10.9 %collective-permute-start.5 = (bf16[4,128,256]{2,1,0:T(8,128)(2,1)S(1)}, bf16[4,128,256]{2,1,0:T(8,128)(2,1)S(1)}, u32[]{:S(2)}, u32[]{:S(2)}) collective-permute-start(bf16[4,128,256]{2,1,0:T(8,128)(2,1)S(1)} %collective-permute-done.3), channel_id=1, source_target_pairs={{0,1},{1,2},{2,3},{3,4},{4,5},{5,6},{6,7},{7,0},{8,9},{9,10},{10,1... | collective-permute-start | bytes 786440 | tf_op jit(solution)/shard_map/ppermute | solution.py:74
  131.2 10.9 %collective-permute-start.6 = (bf16[4,128,256]{2,1,0:T(8,128)(2,1)S(1)}, bf16[4,128,256]{2,1,0:T(8,128)(2,1)S(1)}, u32[]{:S(2)}, u32[]{:S(2)}) collective-permute-start(bf16[4,128,256]{2,1,0:T(8,128)(2,1)S(1)} %collective-permute-done.5), channel_id=1, source_target_pairs={{0,1},{1,2},{2,3},{3,4},{4,5},{5,6},{6,7},{7,0},{8,9},{9,10},{10,1... | collective-permute-start | bytes 786440 | tf_op jit(solution)/shard_map/ppermute | solution.py:74
Sparse Core Ops, SparseCore 0:
  15.4 46.8 all-gather.5
  146.7 19.1 reduce-scatter.1
